TPU v7x, 32 devices: a whole 2x2x4 slice. The times are simulated.
32 devices in a mesh: rows: 8 (over z, x), grp: 4 (over y, core).
Axes of the slice: x: 2, y: 2, z: 4, core: 2. Of those that a mesh axis runs over, the one named last changes fastest.
Arguments:
- user_features: bfloat16 [4, 2048, 256], P('grp', 'rows'), may hold values from -72 to 72
- w_first: bfloat16 [256, 256], replicated, may hold values from -0.375 to 0.375
- w_second: bfloat16 [256, 256], replicated, may hold values from -0.375 to 0.375
- item_embed: bfloat16 [4, 2048, 256], P('grp', 'rows'), may hold values from -27 to 27
- example_weight: float32 [4, 2048], P('grp', 'rows'), may hold values from 0.02 to 0.2
- positive: int32 [4, 2048], P('grp', 'rows'), may hold values from 0 to 2047
- item_owner: int32 [4, 2048, 1], P('grp', 'rows'), may hold values from 0 to 7; in each aligned block of 256 rows (0 to 255, 256 to 511, ..., all dimensions but the last counted through in order) at most 128 rows name the same one
- item_row: int32 [4, 2048], P('grp', 'rows'), may hold values from 0 to 4095
Outputs:
- grad_first: float32 [256, 256], replicated
- grad_second: float32 [256, 256], replicated
- grad_table: float32 [32768, 256], P('rows', 'grp')
Inputs may be any that keep to these rules, and one draw needn't show every extreme that they name: `item_owner`: within the rows of one device (aligned blocks of 256 pairs of a group) no owner is named by more than 128 pairs, a bound that some block reaches.
All inputs are finite; a program needn't handle non-finite values.
Results may differ from a plain program's by a relative error of at most 0.0023.
The roundings to bfloat16 on the way count: a program that leaves them out, or rounds other values in their place, can miss the bound.
Values may be sent and summed in bfloat16 or wider, within the bound.
A program may use at most 128 MiB of HBM per device.

v0:
```python
import jax
import jax.numpy as jnp
from jax import lax
from jax.sharding import PartitionSpec as P

ITEMS_DEV = 4096


def contract_first(left, right):
    return lax.dot_general(
        left, right, (((0,), (0,)), ((), ())), preferred_element_type=jnp.float32
    )


def contract_last(left, right):
    return lax.dot_general(
        left, right, (((1,), (1,)), ((), ())), preferred_element_type=jnp.float32
    )


def body(
    user_features, w_first, w_second, item_embed, example_weight, positive, item_owner, item_row
):
    features = user_features[0]
    own_items = item_embed[0]
    weights = example_weight[0]
    targets = positive[0]
    owners = item_owner[0, :, 0]
    item_rows = item_row[0]
    my_users = features.shape[0]
    feature_width = own_items.shape[1]
    peers = lax.axis_size("rows")
    my_index = lax.axis_index("rows")
    pre_act = jnp.dot(features, w_first, preferred_element_type=jnp.float32)
    hidden = jax.nn.silu(pre_act).astype(jnp.bfloat16)
    user_vecs = jnp.dot(hidden, w_second, preferred_element_type=jnp.float32).astype(jnp.bfloat16)
    gathered = lax.all_gather(own_items, "rows", axis=0, tiled=True)
    group_users = gathered.shape[0]
    scores = contract_last(user_vecs, gathered)
    row_max = jnp.max(scores, axis=1, keepdims=True)
    log_total = row_max + jnp.log(jnp.sum(jnp.exp(scores - row_max), axis=1, keepdims=True))
    columns = lax.broadcasted_iota(jnp.int32, (1, group_users), 1)
    chosen = (columns == targets[:, None]).astype(jnp.float32)
    dscore = (weights[:, None] * (jnp.exp(scores - log_total) - chosen)).astype(jnp.bfloat16)
    grad_user = jnp.dot(dscore, gathered, preferred_element_type=jnp.float32).astype(jnp.bfloat16)
    everyone = lax.all_gather(user_vecs, "rows", axis=0, tiled=True)
    target_all, total_all, weight_all = (
        lax.all_gather(targets.astype(jnp.float32), "rows", axis=0, tiled=True),
        lax.all_gather(log_total[:, 0], "rows", axis=0, tiled=True),
        lax.all_gather(weights, "rows", axis=0, tiled=True),
    )
    back_scores = contract_last(everyone, own_items)
    own_columns = my_index * my_users + lax.broadcasted_iota(jnp.int32, (1, my_users), 1)
    hits = (own_columns == target_all.astype(jnp.int32)[:, None]).astype(jnp.float32)
    back_dscore = (weight_all[:, None] * (jnp.exp(back_scores - total_all[:, None]) - hits)).astype(
        jnp.bfloat16
    )
    grad_item = contract_first(back_dscore, everyone)
    d_second = contract_first(hidden, grad_user)
    back_grad = contract_last(grad_user, w_second)
    sigmoid_pre = jax.nn.sigmoid(pre_act)
    grad_pre = (back_grad * sigmoid_pre * (1.0 + pre_act * (1.0 - sigmoid_pre))).astype(
        jnp.bfloat16
    )
    d_first = contract_first(features, grad_pre)
    grad_first, grad_second = lax.psum((d_first, d_second), ("rows", "grp"))
    capacity = max(2, 4 * my_users // peers)
    member = (owners[:, None] == lax.broadcasted_iota(jnp.int32, (1, peers), 1)).astype(jnp.int32)
    before = jnp.cumsum(member, axis=0) - member
    slot_rank = jnp.sum(before * member, axis=1)
    slots = owners * capacity + slot_rank
    send_grad = jnp.zeros((peers * capacity, feature_width), jnp.float32).at[slots].set(grad_item)
    send_grad = send_grad.reshape(peers, capacity, feature_width)
    send_rows = (
        jnp.full((peers * capacity,), -1.0, jnp.float32)
        .at[slots]
        .set(item_rows.astype(jnp.float32))
    )
    got_grad, got_rows = (
        lax.all_to_all(send_grad, "rows", split_axis=0, concat_axis=0, tiled=True),
        lax.all_to_all(
            send_rows.reshape(peers, capacity), "rows", split_axis=0, concat_axis=0, tiled=True
        ),
    )
    table_rows = got_rows.reshape(-1).astype(jnp.int32)
    table_rows = jnp.where(table_rows >= 0, table_rows, ITEMS_DEV)
    dense_grad = (
        jnp.zeros((ITEMS_DEV, feature_width), jnp.float32)
        .at[table_rows]
        .add(got_grad.reshape(-1, feature_width), mode="drop")
    )
    grad_table = lax.psum_scatter(dense_grad, "grp", scatter_dimension=1, tiled=True)
    return (grad_first, grad_second, grad_table)


def solution(mesh):
    placed = (
        P("grp", "rows", None),
        P(),
        P(),
        P("grp", "rows", None),
        P("grp", "rows"),
        P("grp", "rows"),
        P("grp", "rows", None),
        P("grp", "rows"),
    )
    return jax.shard_map(
        body, mesh=mesh, in_specs=placed, out_specs=(P(), P(), P("rows", "grp")), check_vma=False
    )
```

profile of v0, /device:TPU:0, one launch (start us, length us, event | category | flops | bytes accessed | tf_op | source)
XLA Modules:
  0.0 301.3 jit_solution(13880731240005856503)
XLA Ops:
  7.3 0.7 all-gather.9.cloned.1.call-update
  8.0 1.2 fusion.27
  9.2 0.9 convolution_convert_fusion
  10.1 0.7 convert_element_type.64
  11.7 2.0 scatter_custom_fusion
  13.7 7.3 %all-to-all-start = ((f32[8,1,128]{2,1,0:T(1,128)}), f32[8,1,128]{2,1,0:T(1,128)S(1)}, u32[]{:S(2)}, u32[]{:S(2)}) async-start(f32[8,1,128]{2,1,0:T(1,128)} %bitcast.13), calls=%async_computation | async-start | bytes 8192 | tf_op jit(solution)/shard_map/all_to_all | solution.py:81
  21.0 21.1 %all-gather.3 = f32[8,1,256]{2,1,0:T(1,128)S(1)} all-gather(f32[1,1,256]{2,1,0:T(1,128)S(1)} %bitcast.67), channel_id=1, replica_groups=mesh['rows'=8,'grp'=4] {'rows'}, dimensions={0}, use_global_device_ids=true | all-gather | bytes 9216 | tf_op jit(solution)/shard_map/all_gather | solution.py:48
  42.1 16.3 %all-gather.1 = f32[1,2048]{1,0:T(1,128)S(1)} all-gather(f32[1,256]{1,0:T(1,128)S(1)} %copy-done.4), channel_id=3, replica_groups=mesh['rows'=8,'grp'=4] {'rows'}, dimensions={1}, use_global_device_ids=true | all-gather | bytes 9216 | tf_op jit(solution)/shard_map/all_gather | solution.py:50
  58.4 1.9 fusion.37
  60.7 18.3 %all-gather.2 = f32[8,1,256]{2,1,0:T(1,128)S(1)} all-gather(f32[1,1,256]{2,1,0:T(1,128)S(1)} %bitcast.66), channel_id=1, replica_groups=mesh['rows'=8,'grp'=4] {'rows'}, dimensions={0}, use_global_device_ids=true | all-gather | bytes 9216 | tf_op jit(solution)/shard_map/all_gather | solution.py:49
  79.1 16.1 %all-gather.7.cloned.1.call-done = bf16[2048,256]{1,0:T(8,128)(2,1)} async-done(((bf16[256,256]{1,0:T(8,128)(2,1)}), bf16[2048,256]{1,0:T(8,128)(2,1)}) %all-gather.7.cloned.1.call-update) | async-done | bytes 1048592 | tf_op jit(solution)/shard_map/all_gather | solution.py:46
  95.2 3.9 %fusion.6 = f32[256,256]{1,0:T(8,128)} fusion(bf16[2048,256]{1,0:T(8,128)(2,1)} %all-gather.7.cloned.1.call-done, s32[256]{0:T(256)S(1)} %iota_add_fusion, f32[2048]{0:T(1024)S(1)} %bitcast.64, f32[2048]{0:T(1024)S(1)} %bitcast.63, s32[2048]{0:T(1024)S(1)} %bitcast.65, bf16[1,256,256]{2,1,0:T(8,128)(2,1)S(1)} %copy-done.2), kind=kOutput, calls=%fused_computation.13 | convolution fusion | flops 540016640 | bytes 1467392 | tf_op jit(solution)/shard_map/dot_general | solution.py:10
  99.1 2.9 scatter_custom_fusion.1
  102.0 4.4 %all-to-all-start.1 = ((f32[8,128,256]{2,1,0:T(8,128)}), f32[8,128,256]{2,1,0:T(8,128)}, u32[]{:S(2)}, u32[]{:S(2)}) async-start(f32[8,128,256]{2,1,0:T(8,128)} %bitcast.22), calls=%async_computation.1 | async-start | bytes 2097152 | tf_op jit(solution)/shard_map/all_to_all | solution.py:80
  106.4 0.8 convolution_convert_fusion.1
  107.8 1.0 fusion.36
  108.8 2.1 convolution_bitcast_fusion
  111.0 20.8 %all-to-all-done.1 = f32[8,128,256]{2,1,0:T(8,128)} async-done(((f32[8,128,256]{2,1,0:T(8,128)}), f32[8,128,256]{2,1,0:T(8,128)}, u32[]{:S(2)}, u32[]{:S(2)}) %all-to-all-start.1) | async-done | bytes 1048608 | tf_op jit(solution)/shard_map/all_to_all | solution.py:80
  131.8 8.7 %scatter_custom_fusion.2 = f32[4096,256]{1,0:T(8,128)} fusion(s32[1024]{0:T(1024)S(1)} %bitcast.68, f32[1024,256]{1,0:T(8,128)} %bitcast.23, f32[]{:T(128)} %constant.13.clone.1), kind=kCustom, calls=%fused_computation.8 | custom fusion | flops 262144 | bytes 4194816 | tf_op jit(solution)/shard_map/scatter-add | solution.py:90
  140.5 5.7 %copy.16 = f32[4096,256]{0,1:T(8,128)} copy(f32[4096,256]{1,0:T(8,128)} %scatter_custom_fusion.2) | data formatting | bytes 8388608
  146.2 100.4 %all-reduce.3.cloned.1.call-done = (f32[256,256]{0,1:T(8,128)}, f32[256,256]{1,0:T(8,128)}) async-done(((f32[256,256]{0,1:T(8,128)}, f32[256,256]{1,0:T(8,128)}), (f32[256,256]{0,1:T(8,128)}, f32[256,256]{1,0:T(8,128)})) %all-reduce.3.cloned.1.call-update) | async-done | bytes 524304 | tf_op jit(solution)/shard_map/psum | solution.py:66
  246.5 1.8 copy.14
  248.3 44.8 %reduce-scatter.4.cloned.1.call-done = f32[64,4096]{1,0:T(8,128)} async-done(((f32[256,4096]{1,0:T(8,128)}), f32[64,4096]{1,0:T(8,128)}) %reduce-scatter.4.cloned.1.call-update) | async-done | bytes 1048592
  293.1 1.7 copy.20
  (38 shorter events, 2.3 us)
Async XLA Ops:
  7.2 2.0 copy-start
  7.2 3.6 %copy-start.3 = (s32[1,256,1]{1,2,0:T(1,128)S(1)}, s32[1,256,1]{1,2,0:T(1,128)}, u32[]{:S(2)}) copy-start(s32[1,256,1]{1,2,0:T(1,128)} %param.14) | copy-start | bytes 3076
  7.2 13.8 %copy-start.5 = (s32[1,256]{1,0:T(1,128)S(1)}, s32[1,256]{1,0:T(1,128)}, u32[]{:S(2)}) copy-start(s32[1,256]{1,0:T(1,128)} %param.13) | copy-start | bytes 3076
  7.2 34.9 %copy-start.4 = (f32[1,256]{1,0:T(1,128)S(1)}, f32[1,256]{1,0:T(1,128)}, u32[]{:S(2)}) copy-start(f32[1,256]{1,0:T(1,128)} %param.12) | copy-start | bytes 3076
  7.2 51.2 %all-gather.9.cloned.1.call-start = ((), (), s32[]{:S(2)}) async-start(), calls=%async_computation.4 | async-start | bytes 1179648 | tf_op jit(solution)/shard_map/all_gather | solution.py:37
  7.9 87.2 %all-gather.7.cloned.1.call-start = ((), (), s32[]{:S(2)}) async-start(), calls=%async_computation.3 | async-start | bytes 1179648 | tf_op jit(solution)/shard_map/all_gather | solution.py:46
  13.7 88.3 %all-to-all-start = ((f32[8,1,128]{2,1,0:T(1,128)}), f32[8,1,128]{2,1,0:T(1,128)S(1)}, u32[]{:S(2)}, u32[]{:S(2)}) async-start(f32[8,1,128]{2,1,0:T(1,128)} %bitcast.13), calls=%async_computation | async-start | bytes 8192 | tf_op jit(solution)/shard_map/all_to_all | solution.py:81
  58.4 36.8 %copy-start.2 = (bf16[1,256,256]{2,1,0:T(8,128)(2,1)S(1)}, bf16[1,256,256]{2,1,0:T(8,128)(2,1)}, u32[]{:S(2)}) copy-start(bf16[1,256,256]{2,1,0:T(8,128)(2,1)} %param.11) | copy-start | bytes 393220
  99.1 7.3 %copy-start.1 = (bf16[1,2048,256]{2,1,0:T(8,128)(2,1)S(1)}, bf16[1,2048,256]{2,1,0:T(8,128)(2,1)}, u32[]{:S(2)}) copy-start(bf16[1,2048,256]{2,1,0:T(8,128)(2,1)} %all-gather.9.cloned.1.call-done) | copy-start | bytes 3145732
  102.0 4.4 %copy-start.6 = (s32[1,256]{1,0:T(1,128)S(1)}, s32[1,256]{1,0:T(1,128)}, u32[]{:S(2)}) copy-start(s32[1,256]{1,0:T(1,128)} %param.13) | copy-start | bytes 3076
  102.0 29.8 %all-to-all-start.1 = ((f32[8,128,256]{2,1,0:T(8,128)}), f32[8,128,256]{2,1,0:T(8,128)}, u32[]{:S(2)}, u32[]{:S(2)}) async-start(f32[8,128,256]{2,1,0:T(8,128)} %bitcast.22), calls=%async_computation.1 | async-start | bytes 2097152 | tf_op jit(solution)/shard_map/all_to_all | solution.py:80
  106.3 140.2 %all-reduce.3.cloned.1.call-start = ((), (), s32[]{:S(2)}) async-start(), calls=%async_computation.6 | async-start | bytes 1048576 | tf_op jit(solution)/shard_map/psum | solution.py:66
  107.2 0.6 copy-start.7
  111.0 182.1 %reduce-scatter.4.cloned.1.call-start = ((), (), s32[]{:S(2)}) async-start(), calls=%async_computation.5 | async-start | bytes 5242880
Sparse Core Ops, SparseCore 0:
  10.1 43.2 all-gather.8
  56.1 38.9 all-gather.6
  113.2 133.2 all-reduce.2
  249.5 43.5 reduce-scatter.3
where the time goes:
time: 302 us; the launch traced here: 301 us
  waiting for transfers between devices  183 us (61%)
  blocking collectives  55.7 us (18%)
  local copies, waits for them, and re-layouts  14.9 us (5%)
  between operations  13.9 us (5%)
  starting transfers between devices  11.8 us (4%)
  matrix products  11.7 us (4%)
  other arithmetic  10.6 us (4%)
    psum x1, waiting for transfers between devices, body(): grad_first, grad_second = lax.psum((d_first, d_second), ('rows', 'grp'))  100 us
    unnamed x5, waiting for transfers between devices  45.5 us
    all_gather x1, blocking collectives, body(): lax.all_gather(targets.astype(jnp.float32), 'rows', axis=0, tiled=True)  21.1 us
    all_to_all x1, waiting for transfers between devices, body(): lax.all_to_all(send_grad, 'rows', split_axis=0, concat_axis=0, tiled=True)  20.8 us
    all_gather x1, blocking collectives, body(): lax.all_gather(log_total[:, 0], 'rows', axis=0, tiled=True)  18.3 us
    all_gather x1, blocking collectives, body(): lax.all_gather(weights, 'rows', axis=0, tiled=True)  16.3 us
    all_gather x1, waiting for transfers between devices, body(): everyone = lax.all_gather(user_vecs, 'rows', axis=0, tiled=True)  16.1 us
    unnamed x19, local copies, waits for them, and re-layouts  9.79 us
  transfers between devices with their start and end apart: 6, of which 4 were waited for; matrix products, arithmetic and copies ran while one was open for 12% of the time, Pallas kernels for 0%

commit v1 on v0

--- a/solution.py
+++ b/solution.py
@@ -4,6 +4,17 @@
 from jax.sharding import PartitionSpec as P
 
 ITEMS_DEV = 4096
+
+
+def gather_by_hops(shard, axis, dim):
+    n_dev = lax.axis_size(axis)
+    right = [(i, (i + 1) % n_dev) for i in range(n_dev)]
+    shards = [shard]
+    for far in range(1, n_dev):
+        shards = [lax.ppermute(shards[0], axis, right), *shards]
+    out = jnp.concatenate(shards, axis=dim)
+    shift = (lax.axis_index(axis) + 1) * shards[-1].shape[dim]
+    return jnp.roll(out, shift, axis=dim)
 
 
 def contract_first(left, right):
@@ -43,7 +54,7 @@
     chosen = (columns == targets[:, None]).astype(jnp.float32)
     dscore = (weights[:, None] * (jnp.exp(scores - log_total) - chosen)).astype(jnp.bfloat16)
     grad_user = jnp.dot(dscore, gathered, preferred_element_type=jnp.float32).astype(jnp.bfloat16)
-    everyone = lax.all_gather(user_vecs, "rows", axis=0, tiled=True)
+    everyone = gather_by_hops(user_vecs, "rows", 0)
     target_all, total_all, weight_all = (
         lax.all_gather(targets.astype(jnp.float32), "rows", axis=0, tiled=True),
         lax.all_gather(log_total[:, 0], "rows", axis=0, tiled=True),

time: 302 us -> 341 us (1.13)
  waiting for transfers between devices: 183 us -> 207 us
  local copies, waits for them, and re-layouts: 14.9 us -> 25.3 us
    ppermute x0 -> x7, waiting for transfers between devices: none -> 44.1 us  [gather_by_hops(): shards = [lax.ppermute(shards[0], axis, right), *shards]]
    all_gather x1 -> x0, waiting for transfers between devices: 16.1 us -> none  [body(): everyone = lax.all_gather(user_vecs, 'rows', axis=0, tiled=True)]
    unnamed x19 -> x36, local copies, waits for them, and re-layouts: 9.79 us -> 19.6 us
    all_to_all x1, waiting for transfers between devices: 20.8 us -> 11.7 us  [body(): lax.all_to_all(send_grad, 'rows', split_axis=0, concat_axis=0, tiled=True)]
    psum x1, waiting for transfers between devices: 100 us -> 107 us  [body(): grad_first, grad_second = lax.psum((d_first, d_second), ('rows', 'grp'))]
    unnamed x5 -> x4, waiting for transfers between devices: 45.5 us -> 45 us
  transfers between devices with their start and end apart: 6 -> 12, of which waited for: 4 -> 9; matrix products, arithmetic and copies ran while one was open for 12% -> 13% of each run, Pallas kernels for 0% -> 0%
where the time goes in v1:
time: 341 us; the launch traced here: 340 us
  waiting for transfers between devices  207 us (61%)
  blocking collectives  55.7 us (16%)
  local copies, waits for them, and re-layouts  25.3 us (7%)
  between operations  13.9 us (4%)
  starting transfers between devices  13.4 us (4%)
  other arithmetic  13.3 us (4%)
  matrix products  10.9 us (3%)
    psum x1, waiting for transfers between devices, body(): grad_first, grad_second = lax.psum((d_first, d_second), ('rows', 'grp'))  107 us
    unnamed x4, waiting for transfers between devices  45 us
    ppermute x7, waiting for transfers between devices, gather_by_hops(): shards = [lax.ppermute(shards[0], axis, right), *shards]  44.1 us
    all_gather x1, blocking collectives, body(): lax.all_gather(targets.astype(jnp.float32), 'rows', axis=0, tiled=True)  21.1 us
    unnamed x36, local copies, waits for them, and re-layouts  19.6 us
    all_gather x1, blocking collectives, body(): lax.all_gather(log_total[:, 0], 'rows', axis=0, tiled=True)  18.4 us
    all_gather x1, blocking collectives, body(): lax.all_gather(weights, 'rows', axis=0, tiled=True)  16.3 us
    all_to_all x1, waiting for transfers between devices, body(): lax.all_to_all(send_grad, 'rows', split_axis=0, concat_axis=0, tiled=True)  11.7 us
  transfers between devices with their start and end apart: 12, of which 9 were waited for; matrix products, arithmetic and copies ran while one was open for 13% of the time, Pallas kernels for 0%

profile of v1, /device:TPU:0, one launch (start us, length us, event | category | flops | bytes accessed | tf_op | source)
XLA Modules:
  0.0 340.0 jit_solution(9813257068530009780)
XLA Ops:
  8.6 3.0 collective-permute-start
  11.7 6.5 %collective-permute-done = bf16[256,256]{1,0:T(8,128)(2,1)S(1)} collective-permute-done((bf16[256,256]{1,0:T(8,128)(2,1)S(1)}, bf16[256,256]{1,0:T(8,128)(2,1)S(1)}, u32[]{:S(2)}, u32[]{:S(2)}) %collective-permute-start) | collective-permute-done | bytes 131104 | tf_op jit(solution)/shard_map/ppermute | solution.py:14
  18.2 7.7 %collective-permute-done.1 = bf16[256,256]{1,0:T(8,128)(2,1)S(1)} collective-permute-done((bf16[256,256]{1,0:T(8,128)(2,1)S(1)}, bf16[256,256]{1,0:T(8,128)(2,1)S(1)}, u32[]{:S(2)}, u32[]{:S(2)}) %collective-permute-start.1) | collective-permute-done | bytes 131104 | tf_op jit(solution)/shard_map/ppermute | solution.py:14
  25.9 7.7 %collective-permute-done.2 = bf16[256,256]{1,0:T(8,128)(2,1)S(1)} collective-permute-done((bf16[256,256]{1,0:T(8,128)(2,1)S(1)}, bf16[256,256]{1,0:T(8,128)(2,1)S(1)}, u32[]{:S(2)}, u32[]{:S(2)}) %collective-permute-start.2) | collective-permute-done | bytes 131104 | tf_op jit(solution)/shard_map/ppermute | solution.py:14
  33.6 7.6 %collective-permute-done.3 = bf16[256,256]{1,0:T(8,128)(2,1)S(1)} collective-permute-done((bf16[256,256]{1,0:T(8,128)(2,1)S(1)}, bf16[256,256]{1,0:T(8,128)(2,1)S(1)}, u32[]{:S(2)}, u32[]{:S(2)}) %collective-permute-start.3) | collective-permute-done | bytes 131104 | tf_op jit(solution)/shard_map/ppermute | solution.py:14
  42.4 7.2 %collective-permute-done.4 = bf16[256,256]{1,0:T(8,128)(2,1)S(1)} collective-permute-done((bf16[256,256]{1,0:T(8,128)(2,1)S(1)}, bf16[256,256]{1,0:T(8,128)(2,1)S(1)}, u32[]{:S(2)}, u32[]{:S(2)}) %collective-permute-start.4) | collective-permute-done | bytes 131104 | tf_op jit(solution)/shard_map/ppermute | solution.py:14
  50.7 7.4 %collective-permute-done.5 = bf16[256,256]{1,0:T(8,128)(2,1)S(1)} collective-permute-done((bf16[256,256]{1,0:T(8,128)(2,1)S(1)}, bf16[256,256]{1,0:T(8,128)(2,1)S(1)}, u32[]{:S(2)}, u32[]{:S(2)}) %collective-permute-start.5) | collective-permute-done | bytes 131104 | tf_op jit(solution)/shard_map/ppermute | solution.py:14
  59.5 2.0 scatter_custom_fusion
  61.4 6.0 %all-to-all-start = ((f32[8,1,128]{2,1,0:T(1,128)}), f32[8,1,128]{2,1,0:T(1,128)S(1)}, u32[]{:S(2)}, u32[]{:S(2)}) async-start(f32[8,1,128]{2,1,0:T(1,128)} %bitcast.13), calls=%async_computation | async-start | bytes 8192 | tf_op jit(solution)/shard_map/all_to_all | solution.py:92
  68.1 21.1 %all-gather.3 = f32[8,1,256]{2,1,0:T(1,128)S(1)} all-gather(f32[1,1,256]{2,1,0:T(1,128)S(1)} %bitcast.65), channel_id=1, replica_groups=mesh['rows'=8,'grp'=4] {'rows'}, dimensions={0}, use_global_device_ids=true | all-gather | bytes 9216 | tf_op jit(solution)/shard_map/all_gather | solution.py:59
  89.2 16.3 %all-gather.1 = f32[1,2048]{1,0:T(1,128)S(1)} all-gather(f32[1,256]{1,0:T(1,128)S(1)} %copy-done.6), channel_id=3, replica_groups=mesh['rows'=8,'grp'=4] {'rows'}, dimensions={1}, use_global_device_ids=true | all-gather | bytes 9216 | tf_op jit(solution)/shard_map/all_gather | solution.py:61
  116.0 1.8 fusion.41
  118.3 18.4 %all-gather.2 = f32[8,1,256]{2,1,0:T(1,128)S(1)} all-gather(f32[1,1,256]{2,1,0:T(1,128)S(1)} %bitcast.64), channel_id=1, replica_groups=mesh['rows'=8,'grp'=4] {'rows'}, dimensions={0}, use_global_device_ids=true | all-gather | bytes 9216 | tf_op jit(solution)/shard_map/all_gather | solution.py:60
  136.7 3.8 %fusion.6 = f32[256,256]{1,0:T(8,128)} fusion(s32[256]{0:T(256)S(1)} %iota_add_fusion, f32[2048]{0:T(1024)S(1)} %bitcast.62, bf16[4096,256]{1,0:T(8,128)(2,1)} %constant_dynamic-update-slice_fusion, s32[]{:T(128)S(6)} %select_n.49, f32[2048]{0:T(1024)S(1)} %bitcast.61, s32[2048]{0:T(1024)S(1)} %bitcast.63, bf16[1,256,256]{2,1,0:T(8,128)(2,1)S(1)} %copy-done.4), kind=kOutput, calls=%fused_computation.13 | convolution fusion | flops 540016640 | bytes 2516992 | tf_op jit(solution)/shard_map/dot_general | solution.py:21
  140.5 2.9 scatter_custom_fusion.1
  143.4 4.2 %all-to-all-start.1 = ((f32[8,128,256]{2,1,0:T(8,128)}), f32[8,128,256]{2,1,0:T(8,128)}, u32[]{:S(2)}, u32[]{:S(2)}) async-start(f32[8,128,256]{2,1,0:T(8,128)} %bitcast.22), calls=%async_computation.1 | async-start | bytes 2097152 | tf_op jit(solution)/shard_map/all_to_all | solution.py:91
  150.1 2.2 convolution_bitcast_fusion
  152.4 11.7 %all-to-all-done.1 = f32[8,128,256]{2,1,0:T(8,128)} async-done(((f32[8,128,256]{2,1,0:T(8,128)}), f32[8,128,256]{2,1,0:T(8,128)}, u32[]{:S(2)}, u32[]{:S(2)}) %all-to-all-start.1) | async-done | bytes 1048608 | tf_op jit(solution)/shard_map/all_to_all | solution.py:91
  164.1 8.7 %scatter_custom_fusion.2 = f32[4096,256]{1,0:T(8,128)} fusion(s32[1024]{0:T(1024)S(1)} %bitcast.66, f32[1024,256]{1,0:T(8,128)} %bitcast.23, f32[]{:T(128)} %constant.22.clone.1), kind=kCustom, calls=%fused_computation.8 | custom fusion | flops 262144 | bytes 4194816 | tf_op jit(solution)/shard_map/scatter-add | solution.py:101
  172.8 5.6 %copy.16 = f32[4096,256]{0,1:T(8,128)} copy(f32[4096,256]{1,0:T(8,128)} %scatter_custom_fusion.2) | data formatting | bytes 8388608
  178.4 106.7 %all-reduce.3.cloned.1.call-done = (f32[256,256]{0,1:T(8,128)}, f32[256,256]{1,0:T(8,128)}) async-done(((f32[256,256]{0,1:T(8,128)}, f32[256,256]{1,0:T(8,128)}), (f32[256,256]{0,1:T(8,128)}, f32[256,256]{1,0:T(8,128)})) %all-reduce.3.cloned.1.call-update) | async-done | bytes 524304 | tf_op jit(solution)/shard_map/psum | solution.py:77
  285.1 1.8 copy.14
  286.9 44.9 %reduce-scatter.4.cloned.1.call-done = f32[64,4096]{1,0:T(8,128)} async-done(((f32[256,4096]{1,0:T(8,128)}), f32[64,4096]{1,0:T(8,128)}) %reduce-scatter.4.cloned.1.call-update) | async-done | bytes 1048592
  331.8 1.7 copy.35
  (67 shorter events, 19.3 us)
Async XLA Ops:
  7.2 1.2 copy-start
  7.2 82.0 %copy-start.6 = (f32[1,256]{1,0:T(1,128)S(1)}, f32[1,256]{1,0:T(1,128)}, u32[]{:S(2)}) copy-start(f32[1,256]{1,0:T(1,128)} %param.12) | copy-start | bytes 3076
  7.2 108.8 %all-gather.6.cloned.1.call-start = ((), (), s32[]{:S(2)}) async-start(), calls=%async_computation.3 | async-start | bytes 1179648 | tf_op jit(solution)/shard_map/all_gather | solution.py:48
  8.4 25.1 %copy-start.2 = (f32[256,256]{1,0:T(8,128)}, f32[256,256]{1,0:T(8,128)S(1)}, u32[]{:S(2)}) copy-start(f32[256,256]{1,0:T(8,128)S(1)} %fusion.29) | copy-start | bytes 786436
  8.6 9.6 %collective-permute-start = (bf16[256,256]{1,0:T(8,128)(2,1)S(1)}, bf16[256,256]{1,0:T(8,128)(2,1)S(1)}, u32[]{:S(2)}, u32[]{:S(2)}) collective-permute-start(bf16[256,256]{1,0:T(8,128)(2,1)S(1)} %convolution_convert_fusion), channel_id=1, source_target_pairs={{0,4},{4,8},{8,12},{12,16},{16,20},{20,24},{24,28},{28,0},{1,5},{5... | collective-permute-start | bytes 393224 | tf_op jit(solution)/shard_map/ppermute | solution.py:14
  18.2 7.7 %collective-permute-start.1 = (bf16[256,256]{1,0:T(8,128)(2,1)S(1)}, bf16[256,256]{1,0:T(8,128)(2,1)S(1)}, u32[]{:S(2)}, u32[]{:S(2)}) collective-permute-start(bf16[256,256]{1,0:T(8,128)(2,1)S(1)} %collective-permute-done), channel_id=1, source_target_pairs={{0,4},{4,8},{8,12},{12,16},{16,20},{20,24},{24,28},{28,0},{1,5},{5... | collective-permute-start | bytes 393224 | tf_op jit(solution)/shard_map/ppermute | solution.py:14
  25.9 7.7 %collective-permute-start.2 = (bf16[256,256]{1,0:T(8,128)(2,1)S(1)}, bf16[256,256]{1,0:T(8,128)(2,1)S(1)}, u32[]{:S(2)}, u32[]{:S(2)}) collective-permute-start(bf16[256,256]{1,0:T(8,128)(2,1)S(1)} %collective-permute-done.1), channel_id=1, source_target_pairs={{0,4},{4,8},{8,12},{12,16},{16,20},{20,24},{24,28},{28,0},{1,5},{5... | collective-permute-start | bytes 393224 | tf_op jit(solution)/shard_map/ppermute | solution.py:14
  33.5 7.7 %collective-permute-start.3 = (bf16[256,256]{1,0:T(8,128)(2,1)S(1)}, bf16[256,256]{1,0:T(8,128)(2,1)S(1)}, u32[]{:S(2)}, u32[]{:S(2)}) collective-permute-start(bf16[256,256]{1,0:T(8,128)(2,1)S(1)} %collective-permute-done.2), channel_id=1, source_target_pairs={{0,4},{4,8},{8,12},{12,16},{16,20},{20,24},{24,28},{28,0},{1,5},{5... | collective-permute-start | bytes 393224 | tf_op jit(solution)/shard_map/ppermute | solution.py:14
  41.2 8.5 %collective-permute-start.4 = (bf16[256,256]{1,0:T(8,128)(2,1)S(1)}, bf16[256,256]{1,0:T(8,128)(2,1)S(1)}, u32[]{:S(2)}, u32[]{:S(2)}) collective-permute-start(bf16[256,256]{1,0:T(8,128)(2,1)S(1)} %collective-permute-done.3), channel_id=1, source_target_pairs={{0,4},{4,8},{8,12},{12,16},{16,20},{20,24},{24,28},{28,0},{1,5},{5... | collective-permute-start | bytes 393224 | tf_op jit(solution)/shard_map/ppermute | solution.py:14
  49.6 8.5 %collective-permute-start.5 = (bf16[256,256]{1,0:T(8,128)(2,1)S(1)}, bf16[256,256]{1,0:T(8,128)(2,1)S(1)}, u32[]{:S(2)}, u32[]{:S(2)}) collective-permute-start(bf16[256,256]{1,0:T(8,128)(2,1)S(1)} %collective-permute-done.4), channel_id=1, source_target_pairs={{0,4},{4,8},{8,12},{12,16},{16,20},{20,24},{24,28},{28,0},{1,5},{5... | collective-permute-start | bytes 393224 | tf_op jit(solution)/shard_map/ppermute | solution.py:14
  58.1 47.4 %collective-permute-start.6 = (bf16[256,256]{1,0:T(8,128)(2,1)S(1)}, bf16[256,256]{1,0:T(8,128)(2,1)S(1)}, u32[]{:S(2)}, u32[]{:S(2)}) collective-permute-start(bf16[256,256]{1,0:T(8,128)(2,1)S(1)} %collective-permute-done.5), channel_id=1, source_target_pairs={{0,4},{4,8},{8,12},{12,16},{16,20},{20,24},{24,28},{28,0},{1,5},{5... | collective-permute-start | bytes 393224 | tf_op jit(solution)/shard_map/ppermute | solution.py:14
  61.4 81.9 %all-to-all-start = ((f32[8,1,128]{2,1,0:T(1,128)}), f32[8,1,128]{2,1,0:T(1,128)S(1)}, u32[]{:S(2)}, u32[]{:S(2)}) async-start(f32[8,1,128]{2,1,0:T(1,128)} %bitcast.13), calls=%async_computation | async-start | bytes 8192 | tf_op jit(solution)/shard_map/all_to_all | solution.py:92
  116.0 20.6 %copy-start.4 = (bf16[1,256,256]{2,1,0:T(8,128)(2,1)S(1)}, bf16[1,256,256]{2,1,0:T(8,128)(2,1)}, u32[]{:S(2)}) copy-start(bf16[1,256,256]{2,1,0:T(8,128)(2,1)} %param.11) | copy-start | bytes 393220
  140.5 7.2 %copy-start.1 = (bf16[1,2048,256]{2,1,0:T(8,128)(2,1)S(1)}, bf16[1,2048,256]{2,1,0:T(8,128)(2,1)}, u32[]{:S(2)}) copy-start(bf16[1,2048,256]{2,1,0:T(8,128)(2,1)} %all-gather.6.cloned.1.call-done) | copy-start | bytes 3145732
  140.5 7.2 %copy-start.7 = (s32[1,256]{1,0:T(1,128)S(1)}, s32[1,256]{1,0:T(1,128)}, u32[]{:S(2)}) copy-start(s32[1,256]{1,0:T(1,128)} %param.13) | copy-start | bytes 3076
  143.4 20.7 %all-to-all-start.1 = ((f32[8,128,256]{2,1,0:T(8,128)}), f32[8,128,256]{2,1,0:T(8,128)}, u32[]{:S(2)}, u32[]{:S(2)}) async-start(f32[8,128,256]{2,1,0:T(8,128)} %bitcast.22), calls=%async_computation.1 | async-start | bytes 2097152 | tf_op jit(solution)/shard_map/all_to_all | solution.py:91
  147.6 137.5 %all-reduce.3.cloned.1.call-start = ((), (), s32[]{:S(2)}) async-start(), calls=%async_computation.5 | async-start | bytes 1048576 | tf_op jit(solution)/shard_map/psum | solution.py:77
  147.7 1.4 copy-start.3
  147.7 2.4 copy-start.5
  148.5 0.6 copy-start.8
  152.3 179.5 %reduce-scatter.4.cloned.1.call-start = ((), (), s32[]{:S(2)}) async-start(), calls=%async_computation.4 | async-start | bytes 5242880
Sparse Core Ops, SparseCore 0:
  33.7 44.1 all-gather.5
  154.5 130.5 all-reduce.2
  288.2 43.5 reduce-scatter.3
